TPU v7x, 32 devices: a whole 2x2x4 slice. The times are simulated.
32 devices in a mesh: rep: 8 (over y, x, core), tp: 4 (over z).
Axes of the slice: x: 2, y: 2, z: 4, core: 2. Of those that a mesh axis runs over, the one named last changes fastest.
Arguments:
- tokens: bfloat16 [8192, 1280], P(('rep', 'tp')), may hold values from -6 to 6
- view_ids: int32 [32, 4], P('rep'), may hold values from 0 to 31
- time_ids: int32 [32], P('rep'), may hold values from 0 to 999
- camera_table: float32 [32, 1280], replicated, may hold values from -6 to 6
- norm_attn: float32 [2, 1280], replicated, may hold values from 0.1 to 1.9
- norm_ffn: float32 [2, 1280], replicated, may hold values from 0.1 to 1.9
- w_query: bfloat16 [2, 1280, 1280], P(None, ('rep', 'tp')), may hold values from -0.1677051 to 0.1677051
- w_key: bfloat16 [2, 1280, 1280], P(None, ('rep', 'tp')), may hold values from -6.764106 to 6.764106
- w_value: bfloat16 [2, 1280, 1280], P(None, ('rep', 'tp')), may hold values from -0.15625 to 0.15625
- w_out: bfloat16 [2, 1280, 1280], P(None, ('rep', 'tp')), may hold values from -0.15625 to 0.15625
- w_gate: bfloat16 [2, 1280, 5120], P(None, ('rep', 'tp')), may hold values from -0.15625 to 0.15625
- w_up: bfloat16 [2, 1280, 5120], P(None, ('rep', 'tp')), may hold values from -0.15625 to 0.15625
- w_down: bfloat16 [2, 1280, 5120], P(None, ('rep', 'tp')), may hold values from -0.078125 to 0.078125
Outputs:
- denoised: bfloat16 [8192, 1280], P(('rep', 'tp'))
All inputs are finite; a program needn't handle non-finite values.
Results may differ from a plain program's by a relative error of at most 0.035.
Values may be sent and summed in bfloat16 or wider, within the bound.
A program may use at most 128 MiB of HBM per device.

v0:
```python
import math

import jax
import jax.numpy as jnp
from jax import lax
from jax.sharding import PartitionSpec as P

D = 1280
HEADS = 8
VIEWS = 4
HW = 64
LAYERS = 2


def layer_norm(activations, gain_vector):
    average = jnp.mean(activations, axis=-1, keepdims=True)
    centred = activations - average
    spread = jnp.mean(centred * centred, axis=-1, keepdims=True)
    return (centred * lax.rsqrt(spread + 1e-05) * gain_vector).astype(jnp.bfloat16)


def time_code(step_ids, width):
    half_width = width // 2
    frequency = jnp.exp(-math.log(10000.0) * jnp.arange(half_width, dtype=jnp.float32) / half_width)
    angles = step_ids.astype(jnp.float32)[:, None] * frequency[None, :]
    return jnp.concatenate([jnp.cos(angles), jnp.sin(angles)], axis=1)


def conditioning(row_ids, view_ids, time_ids, camera_table):
    set_ids = row_ids // (VIEWS * HW)
    slot_ids = set_ids * VIEWS + row_ids // HW % VIEWS
    flat_views = view_ids.reshape(-1)
    slot_range = jnp.arange(flat_views.shape[0], dtype=jnp.int32)
    pose_ids = jnp.sum(
        jnp.where(slot_ids[:, None] == slot_range[None, :], flat_views[None, :], 0), axis=1
    )
    set_range = jnp.arange(time_ids.shape[0], dtype=jnp.int32)
    step_ids = jnp.sum(
        jnp.where(set_ids[:, None] == set_range[None, :], time_ids[None, :], 0), axis=1
    )
    pose_range = jnp.arange(camera_table.shape[0], dtype=jnp.int32)
    onehot_pose = (pose_ids[:, None] == pose_range[None, :]).astype(jnp.float32)
    camera = jnp.dot(onehot_pose, camera_table, precision=lax.Precision.HIGHEST)
    return camera + time_code(step_ids, camera_table.shape[1])


def reshard(weights):
    owned = (
        lax.all_to_all(weights[0], "tp", split_axis=2, concat_axis=1, tiled=True),
        lax.all_to_all(weights[1], "tp", split_axis=2, concat_axis=1, tiled=True),
        lax.all_to_all(weights[2], "tp", split_axis=2, concat_axis=1, tiled=True),
        lax.all_to_all(weights[3], "tp", split_axis=2, concat_axis=1, tiled=True),
        lax.all_to_all(weights[4], "tp", split_axis=2, concat_axis=1, tiled=True),
        lax.all_to_all(weights[5], "tp", split_axis=2, concat_axis=1, tiled=True),
        lax.all_to_all(weights[6], "tp", split_axis=2, concat_axis=1, tiled=True),
    )
    return (
        lax.all_gather(owned[0], "rep", axis=1, tiled=True),
        lax.all_gather(owned[1], "rep", axis=1, tiled=True),
        lax.all_gather(owned[2], "rep", axis=1, tiled=True),
        lax.all_gather(owned[3], "rep", axis=1, tiled=True),
        lax.all_gather(owned[4], "rep", axis=1, tiled=True),
        lax.all_gather(owned[5], "rep", axis=1, tiled=True),
        lax.all_gather(owned[6], "rep", axis=1, tiled=True),
    )


def attend(packed, width_local, head_size):
    total_rows = packed.shape[0]
    set_count = total_rows // (VIEWS * HW)
    heads_here = width_local // head_size
    shape_heads = (set_count, VIEWS * HW, heads_here, head_size)
    query_rows = packed[:, :width_local].reshape(shape_heads)
    key_rows = packed[:, width_local : 2 * width_local].reshape(shape_heads)
    value_rows = packed[:, 2 * width_local :].reshape(shape_heads)
    scores = jnp.einsum(
        "bqhd,bkhd->bhqk", query_rows, key_rows, preferred_element_type=jnp.float32
    ) * head_size ** (-0.5)
    peak = jnp.max(scores, axis=-1, keepdims=True)
    expons = jnp.exp(scores - peak)
    attn_probs = (expons / jnp.sum(expons, axis=-1, keepdims=True)).astype(jnp.bfloat16)
    mixed_rows = jnp.einsum(
        "bhqk,bkhd->bqhd", attn_probs, value_rows, preferred_element_type=jnp.float32
    )
    return mixed_rows.astype(jnp.bfloat16).reshape(total_rows, width_local)


def out_terms(mixed_rows, weight):
    return lax.dot_general(
        mixed_rows, weight, (((1,), (1,)), ((), ())), preferred_element_type=jnp.float32
    )


def body(
    tokens,
    view_ids,
    time_ids,
    camera_table,
    norm_attn,
    norm_ffn,
    w_query,
    w_key,
    w_value,
    w_out,
    w_gate,
    w_up,
    w_down,
):
    tp_count = lax.axis_size("tp")
    query_w, key_w, value_w, out_w, gate_w, up_w, down_w = reshard(
        (w_query, w_key, w_value, w_out, w_gate, w_up, w_down)
    )
    width_local = query_w.shape[2]
    head_size = D // HEADS
    share_rows = tokens.shape[0]
    group_total = share_rows * tp_count
    first_row = lax.axis_index("tp") * share_rows
    whole_rows = lax.all_gather(tokens, "tp", axis=0, tiled=True)
    row_ids = jnp.arange(group_total, dtype=jnp.int32)
    stream = whole_rows.astype(jnp.float32) + conditioning(
        row_ids, view_ids, time_ids, camera_table
    )

    def total_terms(partial_value):
        return lax.psum(partial_value.astype(jnp.bfloat16), "tp").astype(jnp.float32)

    for layer_index in range(LAYERS):
        query_here = query_w[layer_index]
        key_here = key_w[layer_index]
        value_here = value_w[layer_index]
        gate_here = gate_w[layer_index]
        up_here = up_w[layer_index]
        normed = layer_norm(stream, norm_attn[layer_index])
        packed = jnp.concatenate(
            [
                jnp.dot(normed, query_here, preferred_element_type=jnp.float32).astype(
                    jnp.bfloat16
                ),
                jnp.dot(normed, key_here, preferred_element_type=jnp.float32).astype(jnp.bfloat16),
                jnp.dot(normed, value_here, preferred_element_type=jnp.float32).astype(
                    jnp.bfloat16
                ),
            ],
            axis=1,
        )
        mixed_rows = attend(packed, width_local, head_size)
        stream = stream + total_terms(out_terms(mixed_rows, out_w[layer_index]))
        normed = layer_norm(stream, norm_ffn[layer_index])
        gate_part = jnp.dot(normed, gate_here, preferred_element_type=jnp.float32)
        up_part = jnp.dot(normed, up_here, preferred_element_type=jnp.float32)
        hidden = (jax.nn.gelu(gate_part, approximate=False) * up_part).astype(jnp.bfloat16)
        stream = stream + total_terms(out_terms(hidden, down_w[layer_index]))
    return lax.dynamic_slice_in_dim(stream, first_row, share_rows, 0).astype(jnp.bfloat16)


def solution(mesh):
    return jax.shard_map(
        body,
        mesh=mesh,
        in_specs=(
            P(("rep", "tp"), None),
            P("rep", None),
            P("rep"),
            P(),
            P(),
            P(),
            P(None, ("rep", "tp"), None),
            P(None, ("rep", "tp"), None),
            P(None, ("rep", "tp"), None),
            P(None, ("rep", "tp"), None),
            P(None, ("rep", "tp"), None),
            P(None, ("rep", "tp"), None),
            P(None, ("rep", "tp"), None),
        ),
        out_specs=P(("rep", "tp"), None),
        check_vma=False,
    )
```

profile of v0, /device:TPU:0, one launch (start us, length us, event | category | flops | bytes accessed | tf_op | source)
XLA Modules:
  0.0 892.5 jit_solution(10918619393631502398)
XLA Ops:
  9.8 13.8 %all_to_all.126 = bf16[4,2,12800]{2,1,0:T(2,128)(2,1)S(1)} all-to-all(bf16[4,2,12800]{2,1,0:T(2,128)(2,1)S(1)} %reshape.139), channel_id=1, replica_groups=mesh['rep'=8,'tp'=4] {'tp'}, dimensions={0} | all-to-all | bytes 409600 | tf_op jit(solution)/shard_map/all_to_all | solution.py:49
  27.8 19.7 %all_to_all.127 = bf16[4,2,12800]{2,1,0:T(2,128)(2,1)S(1)} all-to-all(bf16[4,2,12800]{2,1,0:T(2,128)(2,1)S(1)} %reshape.137), channel_id=1, replica_groups=mesh['rep'=8,'tp'=4] {'tp'}, dimensions={0} | all-to-all | bytes 409600 | tf_op jit(solution)/shard_map/all_to_all | solution.py:50
  51.7 14.9 %all_to_all.128 = bf16[4,2,12800]{2,1,0:T(2,128)(2,1)S(1)} all-to-all(bf16[4,2,12800]{2,1,0:T(2,128)(2,1)S(1)} %reshape.141), channel_id=1, replica_groups=mesh['rep'=8,'tp'=4] {'tp'}, dimensions={0} | all-to-all | bytes 409600 | tf_op jit(solution)/shard_map/all_to_all | solution.py:51
  69.5 1.8 reshape.143
  71.3 4.0 all-to-all-start.3
  75.7 10.5 %multiply_cosine_fusion = (f32[1024,640]{1,0:T(8,128)S(1)}, f32[1024,640]{1,0:T(8,128)}) fusion(f32[640]{0:T(1024)S(1)} %multiply_exponential_fusion, f32[1024]{0:T(1024)S(1)} %convert_element_type.93), kind=kLoop, calls=%fused_computation.60 | loop fusion | flops 655360 | bytes 5249536 | tf_op jit(solution)/shard_map/cos | solution.py:26
  86.3 1.9 reshape.144
  88.2 1.7 copy.116
  91.8 5.1 fusion.139
  100.0 4.8 all-gather.13.cloned.1.call-done
  104.8 3.1 convolution_convert_fusion.10
  107.9 1.8 reshape.124
  109.7 24.3 %all-gather.15.cloned.1.call-done = bf16[2,1280,320]{2,1,0:T(8,128)(2,1)} async-done(((bf16[2,160,320]{2,1,0:T(8,128)(2,1)}), bf16[2,1280,320]{2,1,0:T(8,128)(2,1)}) %all-gather.15.cloned.1.call-update) | async-done | bytes 1638416 | tf_op jit(solution)/shard_map/all_gather | solution.py:59
  133.9 3.1 convolution_convert_fusion.9
  137.0 2.5 reshape.125
  139.5 23.4 %all-gather.11.cloned.1.call-done = bf16[2,1280,320]{2,1,0:T(8,128)(2,1)} async-done(((bf16[2,160,320]{2,1,0:T(8,128)(2,1)}), bf16[2,1280,320]{2,1,0:T(8,128)(2,1)}) %all-gather.11.cloned.1.call-update) | async-done | bytes 1638416 | tf_op jit(solution)/shard_map/all_gather | solution.py:60
  163.0 3.1 convolution_convert_fusion.11
  166.0 1.8 reshape.123
  167.9 3.3 fusion.140
  171.2 2.0 fusion.30
  173.8 18.1 %all-gather.17.cloned.1.call-done = bf16[2,1280,320]{2,1,0:T(8,128)(2,1)} async-done(((bf16[2,160,320]{2,1,0:T(8,128)(2,1)}), bf16[2,1280,320]{2,1,0:T(8,128)(2,1)}) %all-gather.17.cloned.1.call-update) | async-done | bytes 1638416 | tf_op jit(solution)/shard_map/all_gather | solution.py:61
  192.0 4.3 convolution_convert_fusion.3
  196.6 4.7 copy.97
  201.3 5.1 reshape.145
  206.4 47.9 %all_to_all.129 = bf16[4,2,51200]{2,1,0:T(2,128)(2,1)} all-to-all(bf16[4,2,51200]{2,1,0:T(2,128)(2,1)} %reshape.145), channel_id=1, replica_groups=mesh['rep'=8,'tp'=4] {'tp'}, dimensions={0} | all-to-all | bytes 1638400 | tf_op jit(solution)/shard_map/all_to_all | solution.py:53
  254.2 5.0 reshape.146
  259.3 4.3 copy.117
  263.6 2.2 copy.99
  265.8 4.7 copy.100
  270.6 5.1 reshape.147
  275.6 47.5 %all_to_all.130 = bf16[4,2,51200]{2,1,0:T(2,128)(2,1)} all-to-all(bf16[4,2,51200]{2,1,0:T(2,128)(2,1)} %reshape.147), channel_id=1, replica_groups=mesh['rep'=8,'tp'=4] {'tp'}, dimensions={0} | all-to-all | bytes 1638400 | tf_op jit(solution)/shard_map/all_to_all | solution.py:54
  323.2 5.0 reshape.148
  328.2 4.3 copy.118
  332.5 2.1 copy.102
  334.7 4.7 copy.103
  339.4 5.1 reshape.135
  344.5 25.6 %all_to_all.131 = bf16[4,2,51200]{2,1,0:T(2,128)(2,1)} all-to-all(bf16[4,2,51200]{2,1,0:T(2,128)(2,1)} %reshape.135), channel_id=1, replica_groups=mesh['rep'=8,'tp'=4] {'tp'}, dimensions={0} | all-to-all | bytes 1638400 | tf_op jit(solution)/shard_map/all_to_all | solution.py:55
  370.2 5.0 reshape.136
  375.2 4.3 copy.119
  379.5 2.1 copy.105
  381.8 4.0 fusion.42
  385.8 3.7 multiply_reduce_fusion.2
  389.5 2.8 multiply_convert_fusion.2
  392.4 8.8 fusion.26
  401.2 29.3 %all-gather.21.cloned.1.call-done = bf16[2,1280,1280]{2,1,0:T(8,128)(2,1)} async-done(((bf16[2,160,1280]{2,1,0:T(8,128)(2,1)}), bf16[2,1280,1280]{2,1,0:T(8,128)(2,1)}) %all-gather.21.cloned.1.call-update) | async-done | bytes 6553616 | tf_op jit(solution)/shard_map/all_gather | solution.py:63
  430.5 48.4 %all-gather.23.cloned.1.call-done = bf16[2,1280,1280]{2,1,0:T(8,128)(2,1)} async-done(((bf16[2,160,1280]{2,1,0:T(8,128)(2,1)}), bf16[2,1280,1280]{2,1,0:T(8,128)(2,1)}) %all-gather.23.cloned.1.call-update) | async-done | bytes 6553616 | tf_op jit(solution)/shard_map/all_gather | solution.py:64
  478.9 23.3 %convolution_convert_fusion.2 = bf16[1024,1280]{1,0:T(8,128)(2,1)} fusion(bf16[2,1280,1280]{2,1,0:T(8,128)(2,1)} %all-gather.23.cloned.1.call-done, f32[1024,1280]{1,0:T(8,128)} %fusion.26, bf16[1024,1280]{1,0:T(8,128)(2,1)} %multiply_convert_fusion.2, bf16[2,1280,1280]{2,1,0:T(8,128)(2,1)} %all-gather.21.cloned.1.call-done), kind=kOutput, calls=%fused_computation.57 | convolution fusion | flops 6798704640 | bytes 17039360 | tf_op jit(solution)/shard_map/dot_general | solution.py:89
  502.3 104.2 %all-reduce.7.cloned.1.call-done = bf16[1024,1280]{1,0:T(8,128)(2,1)} async-done(((bf16[1024,1280]{1,0:T(8,128)(2,1)}), bf16[1024,1280]{1,0:T(8,128)(2,1)}) %all-reduce.7.cloned.1.call-update) | async-done | bytes 2621456 | tf_op jit(solution)/shard_map/psum | solution.py:125
  606.5 4.2 fusion.138
  614.1 1.9 convolution_convert_fusion.6
  616.1 2.0 reshape.128
  618.1 3.1 convolution_convert_fusion.5
  621.2 2.4 reshape.129
  623.6 3.1 convolution_convert_fusion.7
  626.7 1.8 reshape.127
  628.5 3.3 fusion.145
  631.8 2.1 fusion.31
  634.6 3.1 convolution_convert_fusion.1
  637.8 103.2 %all-reduce.9.cloned.1.call-done = bf16[1024,1280]{1,0:T(8,128)(2,1)} async-done(((bf16[1024,1280]{1,0:T(8,128)(2,1)}), bf16[1024,1280]{1,0:T(8,128)(2,1)}) %all-reduce.9.cloned.1.call-update) | async-done | bytes 2621456 | tf_op jit(solution)/shard_map/psum | solution.py:125
  741.0 3.9 fusion.137
  747.2 7.9 fusion.25
  755.1 24.4 %convolution_convert_fusion = bf16[1024,1280]{1,0:T(8,128)(2,1)} fusion(bf16[2,1280,1280]{2,1,0:T(8,128)(2,1)} %all-gather.23.cloned.1.call-done, f32[1024,1280]{1,0:T(8,128)} %fusion.25, bf16[2,1280,1280]{2,1,0:T(8,128)(2,1)} %all-gather.21.cloned.1.call-done, f32[1024,1280]{1,0:T(8,128)} %copy-done.5, f32[1280]{0:T(1024)S(1)} %get-tuple-element.5, ...), kind=kOutput, calls=%fused_computation.55 | convolution fusion | flops 6803947520 | bytes 19674112 | tf_op jit(solution)/shard_map/dot_general | solution.py:89
  779.4 103.2 %all-reduce.11.cloned.1.call-done = bf16[1024,1280]{1,0:T(8,128)(2,1)} async-done(((bf16[1024,1280]{1,0:T(8,128)(2,1)}), bf16[1024,1280]{1,0:T(8,128)(2,1)}) %all-reduce.11.cloned.1.call-update) | async-done | bytes 2621456 | tf_op jit(solution)/shard_map/psum | solution.py:125
  882.7 2.4 fusion.29
  (106 shorter events, 27.2 us)
Async XLA Ops:
  6.5 85.3 %copy-start = (f32[32,1280]{1,0:T(8,128)S(1)}, f32[32,1280]{1,0:T(8,128)}, u32[]{:S(2)}) copy-start(f32[32,1280]{1,0:T(8,128)} %param.16) | copy-start | bytes 491524
  6.5 19.6 %copy-start.6 = (bf16[2,40,1280]{2,1,0:T(8,128)(2,1)S(1)}, bf16[2,40,1280]{2,1,0:T(8,128)(2,1)}, u32[]{:S(2)}) copy-start(bf16[2,40,1280]{2,1,0:T(8,128)(2,1)} %param.20) | copy-start | bytes 614404
  6.5 43.5 %copy-start.7 = (bf16[2,40,1280]{2,1,0:T(8,128)(2,1)S(1)}, bf16[2,40,1280]{2,1,0:T(8,128)(2,1)}, u32[]{:S(2)}) copy-start(bf16[2,40,1280]{2,1,0:T(8,128)(2,1)} %param.21) | copy-start | bytes 614404
  6.5 85.3 %all-gather.9.cloned.1.call-start = ((), (), s32[]{:S(2)}) async-start(), calls=%async_computation.7 | async-start | bytes 3276800 | tf_op jit(solution)/shard_map/all_gather | solution.py:118
  7.3 97.5 %all-gather.13.cloned.1.call-start = ((), (), s32[]{:S(2)}) async-start(), calls=%async_computation.9 | async-start | bytes 2211840 | tf_op jit(solution)/shard_map/all_gather | solution.py:58
  24.6 44.4 %copy-start.8 = (bf16[2,40,1280]{2,1,0:T(8,128)(2,1)S(1)}, bf16[2,40,1280]{2,1,0:T(8,128)(2,1)}, u32[]{:S(2)}) copy-start(bf16[2,40,1280]{2,1,0:T(8,128)(2,1)} %param.22) | copy-start | bytes 614404
  26.1 107.8 %all-gather.15.cloned.1.call-start = ((), (), s32[]{:S(2)}) async-start(), calls=%async_computation.10 | async-start | bytes 2211840 | tf_op jit(solution)/shard_map/all_gather | solution.py:59
  26.7 48.7 %copy-start.12 = (s32[4]{0:T(128)S(1)}, s32[4]{0:T(128)}, u32[]{:S(2)}) copy-start(s32[4]{0:T(128)} %param.15) | copy-start | bytes 52
  26.7 48.8 %copy-start.11 = (s32[4,4]{1,0:T(4,128)S(1)}, s32[4,4]{1,0:T(4,128)}, u32[]{:S(2)}) copy-start(s32[4,4]{1,0:T(4,128)} %param.14) | copy-start | bytes 196
  26.7 48.9 %copy-start.9 = (f32[2,1280]{1,0:T(2,128)S(1)}, f32[2,1280]{1,0:T(2,128)}, u32[]{:S(2)}) copy-start(f32[2,1280]{1,0:T(2,128)} %param.17) | copy-start | bytes 30724
  50.0 112.9 %all-gather.11.cloned.1.call-start = ((), (), s32[]{:S(2)}) async-start(), calls=%async_computation.8 | async-start | bytes 2211840 | tf_op jit(solution)/shard_map/all_gather | solution.py:60
  71.3 15.0 %all-to-all-start.3 = ((bf16[4,2,12800]{2,1,0:T(2,128)(2,1)}), bf16[4,2,12800]{2,1,0:T(2,128)(2,1)}, u32[]{:S(2)}, u32[]{:S(2)}) async-start(bf16[4,2,12800]{2,1,0:T(2,128)(2,1)} %reshape.143), calls=%async_computation.3 | async-start | bytes 409600 | tf_op jit(solution)/shard_map/all_to_all | solution.py:52
  75.3 116.7 %all-gather.17.cloned.1.call-start = ((), (), s32[]{:S(2)}) async-start(), calls=%async_computation.11 | async-start | bytes 2211840 | tf_op jit(solution)/shard_map/all_gather | solution.py:61
  91.6 290.2 %all-reduce.5.cloned.1.call-start = ((), (), s32[]{:S(2)}) async-start(), calls=%async_computation.12 | async-start | bytes 5242880 | tf_op jit(solution)/shard_map/psum | solution.py:125
  97.0 2.3 copy-start.2
  196.3 196.1 %all-gather.19.cloned.1.call-start = ((), (), s32[]{:S(2)}) async-start(), calls=%async_computation.13 | async-start | bytes 7372800 | tf_op jit(solution)/shard_map/all_gather | solution.py:62
  265.8 164.7 %all-gather.21.cloned.1.call-start = ((), (), s32[]{:S(2)}) async-start(), calls=%async_computation.14 | async-start | bytes 7372800 | tf_op jit(solution)/shard_map/all_gather | solution.py:63
  334.7 144.3 %all-gather.23.cloned.1.call-start = ((), (), s32[]{:S(2)}) async-start(), calls=%async_computation.15 | async-start | bytes 7372800 | tf_op jit(solution)/shard_map/all_gather | solution.py:64
  344.5 37.2 %copy-start.10 = (f32[2,1280]{1,0:T(2,128)S(1)}, f32[2,1280]{1,0:T(2,128)}, u32[]{:S(2)}) copy-start(f32[2,1280]{1,0:T(2,128)} %param.18) | copy-start | bytes 30724
  381.6 224.9 %all-reduce.7.cloned.1.call-start = ((), (), s32[]{:S(2)}) async-start(), calls=%async_computation.16 | async-start | bytes 5242880 | tf_op jit(solution)/shard_map/psum | solution.py:125
  381.8 4.1 copy-start.4
  381.8 7.7 slice-start
  385.8 3.7 slice-start.1
  502.3 238.7 %all-reduce.9.cloned.1.call-start = ((), (), s32[]{:S(2)}) async-start(), calls=%async_computation.17 | async-start | bytes 5242880 | tf_op jit(solution)/shard_map/psum | solution.py:125
  610.7 2.3 copy-start.3
  611.4 2.7 copy-start.13
  631.8 2.7 copy-start.14
  637.8 244.9 %all-reduce.11.cloned.1.call-start = ((), (), s32[]{:S(2)}) async-start(), calls=%async_computation.18 | async-start | bytes 5242880 | tf_op jit(solution)/shard_map/psum | solution.py:125
  744.9 2.3 copy-start.5
  755.0 130.1 %copy-start.1 = (f32[32,1280]{1,0:T(8,128)S(1)}, f32[32,1280]{1,0:T(8,128)}, u32[]{:S(2)}) copy-start(f32[32,1280]{1,0:T(8,128)} %param.16) | copy-start | bytes 491524
Sparse Core Ops, SparseCore 0:
  8.9 66.1 all-gather.8
  77.0 27.7 all-gather.12
  106.7 27.2 all-gather.14
  135.7 27.2 all-gather.10
  164.7 27.2 all-gather.16
  196.4 138.2 all-reduce.4
  336.6 45.3 all-gather.18
  384.0 46.4 all-gather.20
  432.4 46.4 all-gather.22
  502.4 104.0 all-reduce.6
  637.9 103.0 all-reduce.8
  779.6 103.0 all-reduce.10
where the time goes:
time: 902 us; the launch traced here: 892 us
  waiting for transfers between devices  460 us (51%)
  blocking collectives  169 us (19%)
  matrix products  105 us (12%)
  local copies, waits for them, and re-layouts  103 us (11%)
  other arithmetic  35.2 us (4%)
  between operations  14.7 us (2%)
    psum x4, waiting for transfers between devices, total_terms(): lax.psum(partial_value.astype(jnp.bfloat16), 'tp').astype(jnp.float32)  311 us
    unnamed x57, local copies, waits for them, and re-layouts  62.7 us
    dot_general x4, matrix products, out_terms(): lax.dot_general(mixed_rows, weight, (((1,), (1,)), ((), ())), preferred_e...  55.2 us
    all_gather x1, waiting for transfers between devices, reshard(): lax.all_gather(owned[6], 'rep', axis=1, tiled=True)  48.4 us
    all_to_all x1, blocking collectives, reshard(): lax.all_to_all(weights[4], 'tp', split_axis=2, concat_axis=1, tiled=True)  47.9 us
    all_to_all x1, blocking collectives, reshard(): lax.all_to_all(weights[5], 'tp', split_axis=2, concat_axis=1, tiled=True)  47.5 us
    all_gather x1, waiting for transfers between devices, reshard(): lax.all_gather(owned[5], 'rep', axis=1, tiled=True)  29.3 us
    all_to_all x1, blocking collectives, reshard(): lax.all_to_all(weights[6], 'tp', split_axis=2, concat_axis=1, tiled=True)  25.6 us
  transfers between devices with their start and end apart: 13, of which 9 were waited for; matrix products, arithmetic and copies ran while one was open for 16% of the time, Pallas kernels for 0%

commit v1 on v0

v1 whole, which is shorter than its diff:
```python
import functools
import math

import jax
import jax.numpy as jnp
from jax import lax
from jax.experimental import pallas as pl
from jax.experimental.pallas import tpu as pltpu
from jax.sharding import PartitionSpec as P

D = 1280
HEADS = 8
VIEWS = 4
HW = 64
LAYERS = 2


def layer_norm(activations, gain_vector):
    average = jnp.mean(activations, axis=-1, keepdims=True)
    centred = activations - average
    spread = jnp.mean(centred * centred, axis=-1, keepdims=True)
    return (centred * lax.rsqrt(spread + 1e-05) * gain_vector).astype(jnp.bfloat16)


def time_code(step_ids, width):
    half_width = width // 2
    frequency = jnp.exp(-math.log(10000.0) * jnp.arange(half_width, dtype=jnp.float32) / half_width)
    angles = step_ids.astype(jnp.float32)[:, None] * frequency[None, :]
    return jnp.concatenate([jnp.cos(angles), jnp.sin(angles)], axis=1)


def conditioning(row_ids, view_ids, time_ids, camera_table):
    set_ids = row_ids // (VIEWS * HW)
    slot_ids = set_ids * VIEWS + row_ids // HW % VIEWS
    flat_views = view_ids.reshape(-1)
    slot_range = jnp.arange(flat_views.shape[0], dtype=jnp.int32)
    pose_ids = jnp.sum(
        jnp.where(slot_ids[:, None] == slot_range[None, :], flat_views[None, :], 0), axis=1
    )
    set_range = jnp.arange(time_ids.shape[0], dtype=jnp.int32)
    step_ids = jnp.sum(
        jnp.where(set_ids[:, None] == set_range[None, :], time_ids[None, :], 0), axis=1
    )
    pose_range = jnp.arange(camera_table.shape[0], dtype=jnp.int32)
    onehot_pose = (pose_ids[:, None] == pose_range[None, :]).astype(jnp.float32)
    camera = jnp.dot(onehot_pose, camera_table, precision=lax.Precision.HIGHEST)
    return camera + time_code(step_ids, camera_table.shape[1])


CLASSES = (("xyz", 9), ("yxz", 9), ("zxy", 31), ("zyx", 31))


def class_columns(width):
    total = sum(share for _, share in CLASSES)
    lanes = width // 128
    bounds, spent = [0], 0
    for _, share in CLASSES:
        spent += share
        bounds.append(lanes * spent // total * 128)
    return [(bounds[i], bounds[i + 1] - bounds[i]) for i in range(len(CLASSES))]


def routes(lengths):
    found = []
    for kind, (order, _) in enumerate(CLASSES):
        spans = {axis: range(1 - lengths[axis], lengths[axis]) for axis in "yz"}
        spans["x"] = range(0, 2)
        for dx in spans["x"]:
            for dy in spans["y"]:
                for dz in spans["z"]:
                    hops = abs(dx) + abs(dy) + abs(dz)
                    found.append((hops, kind, {"x": dx, "y": dy, "z": dz}))
    found.sort(key=lambda item: item[0])
    return found


def send_plan(lengths):
    plan = []
    for hops, kind, offset in routes(lengths):
        order = CLASSES[kind][0]
        last = max([i for i in range(3) if offset[order[i]] != 0], default=-1)
        targets = []
        if last >= 0 and order[last] != "x":
            targets.append((order[last], 1 if offset[order[last]] < 0 else -1))
        for axis in order[last + 1 :]:
            targets += [("x", 1)] if axis == "x" else [(axis, 1), (axis, -1)]
        targets.append(("core", 1))
        plan.append((hops, kind, offset, targets))
    return plan


def gather_kernel(lengths, layers, packed_ref, *refs):
    full_refs = refs[:layers]
    own_sem, send_sems, recv_sems = refs[layers:]
    tp_count = lengths["z"]
    rep_here = lax.axis_index("rep")
    here = {
        "z": lax.axis_index("tp"),
        "y": rep_here // 4,
        "x": rep_here // 2 % 2,
        "core": rep_here % 2,
    }
    columns = class_columns(packed_ref.shape[2])

    def device(place):
        return (place["y"] * 4 + place["x"] * 2 + place["core"], place["z"])

    def moved(place, axis, step):
        place = dict(place)
        place[axis] = 1 - place[axis] if axis in ("x", "core") else place[axis] + step
        return place

    def exists(axis, step):
        if axis in ("x", "core"):
            return None
        return here[axis] < lengths[axis] - 1 if step > 0 else here[axis] > 0

    def both(first, second):
        if first is None or second is None:
            return second if first is None else first
        return jnp.logical_and(first, second)

    def guarded(condition, action):
        if condition is None:
            action()
        else:
            pl.when(condition)(action)

    barrier = pltpu.get_barrier_semaphore()
    neighbours = [("core", 1), ("x", 1), ("y", 1), ("y", -1), ("z", 1), ("z", -1)]
    for axis, step in neighbours:
        def greet(axis=axis, step=step):
            pl.semaphore_signal(
                barrier, inc=1, device_id=device(moved(here, axis, step)),
                device_id_type=pl.DeviceIdType.MESH,
            )
        guarded(exists(axis, step), greet)
    count = jnp.int32(2)
    for axis in "yz":
        count = count + (here[axis] > 0).astype(jnp.int32)
        count = count + (here[axis] < lengths[axis] - 1).astype(jnp.int32)
    pl.semaphore_wait(barrier, count)

    my_rep, my_tp = device(here)
    own_copies = [
        pltpu.make_async_copy(
            packed_ref.at[layer], full_refs[layer].at[my_rep * tp_count + my_tp], own_sem.at[layer]
        )
        for layer in range(layers)
    ]
    for copy in own_copies:
        copy.start()

    finish = []
    plan = send_plan(lengths)

    def run(layer, item):
        hops, kind, offset, targets = item
        start, size = columns[kind]
        source = dict(here)
        valid = None
        for axis in "yz":
            source[axis] = here[axis] + offset[axis]
            if offset[axis] > 0:
                valid = both(valid, source[axis] < lengths[axis])
            elif offset[axis] < 0:
                valid = both(valid, source[axis] >= 0)
        if offset["x"]:
            source["x"] = 1 - here["x"]
        rep_from, tp_from = device(source)
        block = rep_from * tp_count + tp_from
        span = pl.ds(start, size)
        landed = full_refs[layer].at[block, :, span]
        origin = packed_ref.at[layer, :, span] if hops == 0 else landed
        arrived = recv_sems.at[layer * len(CLASSES) + kind, block]
        sends = []
        for axis, step in targets:
            copy = pltpu.make_async_remote_copy(
                src_ref=origin,
                dst_ref=landed,
                send_sem=send_sems.at[len(finish) + len(sends)],
                recv_sem=arrived,
                device_id=device(moved(here, axis, step)),
                device_id_type=pl.DeviceIdType.MESH,
            )
            sends.append((both(valid, exists(axis, step)), copy, exists(axis, step)))

        def action():
            if hops:
                sends[-1][1].wait_recv()
            for _, copy, there in sends:
                guarded(there, copy.start)

        guarded(valid, action)
        finish.extend((condition, copy.wait_send) for condition, copy, _ in sends)

        def from_sibling():
            other = dict(source)
            other["core"] = 1 - here["core"]
            rep_other, tp_other = device(other)
            block_other = rep_other * tp_count + tp_other
            there = full_refs[layer].at[block_other, :, span]
            pltpu.make_async_remote_copy(
                src_ref=there,
                dst_ref=there,
                send_sem=send_sems.at[0],
                recv_sem=recv_sems.at[layer * len(CLASSES) + kind, block_other],
                device_id=device(moved(here, "core", 1)),
                device_id_type=pl.DeviceIdType.MESH,
            ).wait_recv()

        finish.append((valid, from_sibling))

    own = [item for item in plan if item[0] == 0]
    rest = [item for item in plan if item[0] > 0]
    for item in own:
        run(0, item)
    for layer in range(layers):
        early = len(rest) // 2
        for item in rest[:early]:
            run(layer, item)
        if layer + 1 < layers:
            for item in own:
                run(layer + 1, item)
        for item in rest[early:]:
            run(layer, item)
    for condition, action in finish:
        guarded(condition, action)
    for copy in own_copies:
        copy.wait()


def gather_weights(packed, rep_count, tp_count):
    layers, rows, width = packed.shape
    devices = rep_count * tp_count
    lengths = {"x": 2, "y": rep_count // 4, "z": tp_count}
    slots = layers * sum(len(item[3]) + 1 for item in send_plan(lengths))
    full = pl.pallas_call(
        functools.partial(gather_kernel, lengths, layers),
        out_shape=[jax.ShapeDtypeStruct((devices, rows, width), packed.dtype)] * layers,
        in_specs=[pl.BlockSpec(memory_space=pltpu.VMEM)],
        out_specs=[pl.BlockSpec(memory_space=pl.ANY)] * layers,
        scratch_shapes=[
            pltpu.SemaphoreType.DMA((layers,)),
            pltpu.SemaphoreType.DMA((slots,)),
            pltpu.SemaphoreType.DMA((layers * len(CLASSES), devices)),
        ],
        compiler_params=pltpu.CompilerParams(collective_id=0, has_side_effects=True),
        name="gather_weights",
    )(packed)
    return [one.reshape(devices * rows, width) for one in full]


def attend(packed, head_size):
    total_rows = packed.shape[0]
    width = packed.shape[1] // 3
    set_rows = VIEWS * HW
    query_rows, sources = packed[:, :width], packed[:, width:]
    if total_rows % set_rows != 0:
        first = lax.axis_index("tp") * total_rows // set_rows * set_rows
        sources = lax.all_gather(sources, "tp", axis=0, tiled=True)
        sources = lax.dynamic_slice_in_dim(sources, first, set_rows, 0)
    set_count = sources.shape[0] // set_rows
    query_rows = query_rows.reshape(set_count, -1, width // head_size, head_size)
    key_rows = sources[:, :width].reshape(set_count, set_rows, -1, head_size)
    value_rows = sources[:, width:].reshape(set_count, set_rows, -1, head_size)
    scores = jnp.einsum(
        "bqhd,bkhd->bhqk", query_rows, key_rows, preferred_element_type=jnp.float32
    ) * head_size ** (-0.5)
    peak = jnp.max(scores, axis=-1, keepdims=True)
    expons = jnp.exp(scores - peak)
    attn_probs = (expons / jnp.sum(expons, axis=-1, keepdims=True)).astype(jnp.bfloat16)
    mixed_rows = jnp.einsum(
        "bhqk,bkhd->bqhd", attn_probs, value_rows, preferred_element_type=jnp.float32
    )
    return mixed_rows.astype(jnp.bfloat16).reshape(total_rows, width)


def out_terms(mixed_rows, weight):
    return lax.dot_general(
        mixed_rows, weight, (((1,), (1,)), ((), ())), preferred_element_type=jnp.float32
    )


def body(
    tokens,
    view_ids,
    time_ids,
    camera_table,
    norm_attn,
    norm_ffn,
    w_query,
    w_key,
    w_value,
    w_out,
    w_gate,
    w_up,
    w_down,
):
    tp_count = lax.axis_size("tp")
    rep_count = lax.axis_size("rep")
    width = w_query.shape[2]
    inner = w_gate.shape[2]
    head_size = D // HEADS
    shards = (w_query, w_key, w_value, w_out, w_gate, w_up, w_down)
    one_kernel = rep_count % 4 == 0 and rep_count * tp_count * LAYERS * len(CLASSES) <= 256
    if one_kernel:
        weights = gather_weights(jnp.concatenate(shards, axis=2), rep_count, tp_count)
    share_rows = tokens.shape[0]
    row_ids = lax.axis_index("tp") * share_rows + jnp.arange(share_rows, dtype=jnp.int32)
    stream = tokens.astype(jnp.float32) + conditioning(row_ids, view_ids, time_ids, camera_table)

    def whole_weight(layer_index, first, count, after):
        if one_kernel:
            start = sum(shard.shape[2] for shard in shards[:first])
            size = sum(shard.shape[2] for shard in shards[first : first + count])
            return weights[layer_index][:, start : start + size]
        own = [shard[layer_index] for shard in shards[first : first + count]]
        own, _ = lax.optimization_barrier((own, after))
        return lax.all_gather(jnp.concatenate(own, axis=1), ("rep", "tp"), axis=0, tiled=True)

    for layer_index in range(LAYERS):
        normed = layer_norm(stream, norm_attn[layer_index])
        qkv_w = whole_weight(layer_index, 0, 3, normed)
        packed = jnp.dot(normed, qkv_w, preferred_element_type=jnp.float32).astype(jnp.bfloat16)
        mixed_rows = attend(packed, head_size)
        stream = stream + out_terms(mixed_rows, whole_weight(layer_index, 3, 1, mixed_rows))
        normed = layer_norm(stream, norm_ffn[layer_index])
        gate_w = whole_weight(layer_index, 4, 1, normed)
        gate_part = jnp.dot(normed, gate_w, preferred_element_type=jnp.float32)
        up_w = whole_weight(layer_index, 5, 1, gate_part)
        up_part = jnp.dot(normed, up_w, preferred_element_type=jnp.float32)
        hidden = (jax.nn.gelu(gate_part, approximate=False) * up_part).astype(jnp.bfloat16)
        stream = stream + out_terms(hidden, whole_weight(layer_index, 6, 1, hidden))
    return stream.astype(jnp.bfloat16)


def solution(mesh):
    return jax.shard_map(
        body,
        mesh=mesh,
        in_specs=(
            P(("rep", "tp"), None),
            P("rep", None),
            P("rep"),
            P(),
            P(),
            P(),
            P(None, ("rep", "tp"), None),
            P(None, ("rep", "tp"), None),
            P(None, ("rep", "tp"), None),
            P(None, ("rep", "tp"), None),
            P(None, ("rep", "tp"), None),
            P(None, ("rep", "tp"), None),
            P(None, ("rep", "tp"), None),
        ),
        out_specs=P(("rep", "tp"), None),
        check_vma=False,
    )
```

time: 902 us -> 512 us (0.57)
  waiting for transfers between devices: 460 us -> 0 us
  Pallas kernels: 0 us -> 386 us
  blocking collectives: 169 us -> 0 us
  local copies, waits for them, and re-layouts: 103 us -> 11.6 us
  other arithmetic: 35.2 us -> 4.39 us
  between operations: 14.7 us -> 0.65 us
    pallas_call x0 -> x1, Pallas kernels: none -> 386 us  [gather_weights(): pl.pallas_call(functools.partial(gather_kernel, lengths, layers), out_sha...]
    psum x4 -> x0, waiting for transfers between devices: 311 us -> none  [total_terms(): lax.psum(partial_value.astype(jnp.bfloat16), 'tp').astype(jnp.float32)]
    all_to_all x6 -> x0, blocking collectives: 169 us -> none  [the longest x1 47.9 us: reshard(): lax.all_to_all(weights[4], 'tp', split_axis=2, concat_axis=1, tiled=True)]
    all_gather x8 -> x0, waiting for transfers between devices: 148 us -> none  [the longest x1 48.4 us: reshard(): lax.all_gather(owned[6], 'rep', axis=1, tiled=True)]
    unnamed x57 -> x24, local copies, waits for them, and re-layouts: 62.7 us -> 4.76 us
    all_to_all x14 -> x0, local copies, waits for them, and re-layouts: 27 us -> none  [the longest x2 6.48 us: reshard(): lax.all_to_all(weights[4], 'tp', split_axis=2, concat_axis=1, tiled=True)]
    reshape x6 -> x0, local copies, waits for them, and re-layouts: 12.4 us -> none  [the longest x2 4.95 us: attend(): key_rows = packed[:, width_local:2 * width_local].reshape(shape_heads)]
    reduce_sum x3 -> x0, other arithmetic: 12.1 us -> none  [layer_norm(): average = jnp.mean(activations, axis=-1, keepdims=True)]
  transfers between devices with their start and end apart: 13 -> 0, of which waited for: 9 -> 0; matrix products, arithmetic and copies ran while one was open for 16% -> 0% of each run, Pallas kernels for 0% -> 0%
where the time goes in v1:
time: 512 us; the launch traced here: 503 us
  Pallas kernels  386 us (75%)
  matrix products  99.7 us (19%)
  local copies, waits for them, and re-layouts  11.6 us (2%)
    pallas_call x1, Pallas kernels, gather_weights(): pl.pallas_call(functools.partial(gather_kernel, lengths, layers), out_sha...  386 us
    dot_general x4, matrix products, out_terms(): lax.dot_general(mixed_rows, weight, (((1,), (1,)), ((), ())), preferred_e...  52.4 us
    dot_general x2, matrix products, body(): gate_part = jnp.dot(normed, gate_w, preferred_element_type=jnp.float32)  21.7 us
    dot_general x2, matrix products, body(): jnp.dot(normed, qkv_w, preferred_element_type=jnp.float32)  13.2 us

profile of v1, /device:TPU:0, one launch (start us, length us, event | category | flops | bytes accessed | tf_op | source)
XLA Modules:
  0.0 502.5 jit_solution(12548844687635222913)
XLA Ops:
  0.0 0.0 copy-start
  0.0 0.0 copy-start.3
  0.0 0.0 copy-start.2
  0.0 0.0 copy-start.6
  0.0 0.0 copy-start.5
  0.0 0.9 broadcast_in_dim.26
  0.9 0.0 copy-start.7
  0.9 0.0 copy-start.8
  1.0 0.8 select_reduce_fusion.1
  1.8 0.1 select_reduce_fusion
  1.9 0.8 slice_reduce_fusion.1
  2.7 0.8 slice_reduce_fusion
  3.5 0.0 copy-start.4
  3.5 2.3 multiply_cosine_fusion
  5.8 0.0 copy-done
  5.9 2.0 fusion.340
  7.8 0.3 multiply_reduce_fusion.5
  8.1 0.0 copy-done.5
  8.2 0.7 constant_dynamic-update-slice_fusion.6
  8.9 0.0 copy-done.6
  8.9 0.7 constant_dynamic-update-slice_fusion.5
  9.6 0.0 copy-done.7
  9.6 0.7 constant_dynamic-update-slice_fusion.4
  10.3 0.0 copy-done.8
  10.3 0.7 constant_dynamic-update-slice_fusion.3
  11.0 0.0 copy-done.2
  11.0 0.9 constant_dynamic-update-slice_fusion.2
  11.9 0.0 copy-done.3
  11.9 1.0 constant_dynamic-update-slice_fusion.1
  12.9 0.0 copy-done.4
  12.9 0.9 constant_dynamic-update-slice_fusion.packed_ref
  13.8 386.2 %gather_weights.1 = (bf16[32,40,20480]{2,1,0:T(8,128)(2,1)}, bf16[32,40,20480]{2,1,0:T(8,128)(2,1)}) custom-call(bf16[2,40,20480]{2,1,0:T(8,128)(2,1)} %constant_dynamic-update-slice_fusion.packed_ref), custom_call_target="tpu_custom_call" | custom-call | tf_op jit(solution)/shard_map/gather_weights/pallas_call | solution.py:238
  400.0 6.6 %fusion.148 = bf16[256,3840]{1,0:T(8,128)(2,1)S(1)} fusion(bf16[1280,20480]{1,0:T(8,128)(2,1)} %bitcast.37, f32[256,1280]{1,0:T(8,128)S(1)} %get-tuple-element.22, f32[1280]{0:T(1024)S(1)} %get-tuple-element.12, f32[256]{0:T(256)S(1)} %add_rsqrt_fusion.3, f32[256]{0:T(256)S(1)} %broadcast_multiply_fusion.3), kind=kOutput, calls=%fused_computation.148 | convolution fusion | flops 2518876160 | bytes 13114368 | tf_op jit(solution)/shard_map/dot_general | solution.py:325
  406.6 0.1 fusion.339
  406.8 1.1 copy.32
  407.9 0.2 copy.31
  408.1 0.2 copy.30
  408.3 3.3 fusion.341
  411.6 1.9 convolution_convert_fusion.1
  413.5 3.1 fusion.342
  416.6 0.3 multiply_reduce_fusion.4
  416.9 11.0 %fusion.12 = f32[256,5120]{1,0:T(8,128)} fusion(bf16[1280,20480]{1,0:T(8,128)(2,1)} %bitcast.39, f32[256,1280]{1,0:T(8,128)S(1)} %get-tuple-element.26, f32[1280]{0:T(1024)S(1)} %get-tuple-element.10, f32[256]{0:T(256)S(1)} %add_rsqrt_fusion.2, f32[256]{0:T(256)S(1)} %broadcast_multiply_fusion.2), kind=kOutput, calls=%fused_computation.12 | convolution fusion | flops 3356753920 | bytes 19667968 | tf_op jit(solution)/shard_map/dot_general | solution.py:330
  427.9 22.8 %fusion.343 = (f32[256]{0:T(256)S(1)}, f32[256,1280]{1,0:T(8,128)S(1)}) fusion(f32[256,1280]{1,0:T(8,128)S(1)} %get-tuple-element.26, bf16[1280,20480]{1,0:T(8,128)(2,1)} %bitcast.40, f32[256,5120]{1,0:T(8,128)} %fusion.12, f32[1280]{0:T(1024)S(1)} %get-tuple-element.10, f32[256]{0:T(256)S(1)} %add_rsqrt_fusion.2, f32[256]{0:T(256)S(1)} %broadcast_multiply_fusion.2), kind=kOutput, calls=%fused_computation.371 | convolution fusion | flops 6799360000 | bytes 35400704 | tf_op jit(solution)/shard_map/dot_general | solution.py:280
  450.6 0.3 multiply_reduce_fusion.3
  450.9 6.6 %fusion.151 = bf16[256,3840]{1,0:T(8,128)(2,1)S(1)} fusion(bf16[1280,20480]{1,0:T(8,128)(2,1)} %bitcast.33, f32[256,1280]{1,0:T(8,128)S(1)} %get-tuple-element.28, f32[1280]{0:T(1024)S(1)} %get-tuple-element.11, f32[256]{0:T(256)S(1)} %add_rsqrt_fusion.1, f32[256]{0:T(256)S(1)} %broadcast_multiply_fusion.1), kind=kOutput, calls=%fused_computation.149 | convolution fusion | flops 2518876160 | bytes 13114368 | tf_op jit(solution)/shard_map/dot_general | solution.py:325
  457.5 0.1 fusion.338
  457.7 1.1 copy.36
  458.8 0.2 copy.35
  459.0 0.2 copy.34
  459.2 3.3 fusion.346
  462.5 1.9 convolution_convert_fusion
  464.5 3.1 fusion.347
  467.6 0.3 multiply_reduce_fusion.2
  467.9 10.7 %fusion.6 = f32[256,5120]{1,0:T(8,128)} fusion(bf16[1280,20480]{1,0:T(8,128)(2,1)} %bitcast.35, f32[256,1280]{1,0:T(8,128)S(1)} %get-tuple-element.32, f32[1280]{0:T(1024)S(1)} %get-tuple-element.9, f32[256]{0:T(256)S(1)} %add_rsqrt_fusion, f32[256]{0:T(256)S(1)} %broadcast_multiply_fusion), kind=kOutput, calls=%fused_computation.6 | convolution fusion | flops 3356753920 | bytes 19667968 | tf_op jit(solution)/shard_map/dot_general | solution.py:330
  478.6 0.0 copy-start.1
  478.6 23.5 %fusion.235 = bf16[256,1280]{1,0:T(8,128)(2,1)} fusion(f32[256,1280]{1,0:T(8,128)S(1)} %get-tuple-element.32, bf16[1280,20480]{1,0:T(8,128)(2,1)} %bitcast.36, f32[256,5120]{1,0:T(8,128)} %fusion.6, f32[1280]{0:T(1024)S(1)} %get-tuple-element.9, f32[256]{0:T(256)S(1)} %add_rsqrt_fusion, f32[256]{0:T(256)S(1)} %broadcast_multiply_fusion), kind=kOutput, calls=%fused_computation.220 | convolution fusion | flops 6799360000 | bytes 34744320 | tf_op jit(solution)/shard_map/dot_general | solution.py:280
  502.1 0.0 copy-done.1
  (11 shorter events, 0.1 us)
Async XLA Ops:
  0.0 5.9 %copy-start = (f32[32,1280]{1,0:T(8,128)S(1)}, f32[32,1280]{1,0:T(8,128)}, u32[]{:S(2)}) copy-start(f32[32,1280]{1,0:T(8,128)} %param.16) | copy-start | bytes 491524
  0.0 11.9 %copy-start.3 = (bf16[2,40,5120]{2,1,0:T(8,128)(2,1)S(1)}, bf16[2,40,5120]{2,1,0:T(8,128)(2,1)}, u32[]{:S(2)}) copy-start(bf16[2,40,5120]{2,1,0:T(8,128)(2,1)} %param.24) | copy-start | bytes 2457604
  0.0 11.0 %copy-start.2 = (bf16[2,40,5120]{2,1,0:T(8,128)(2,1)S(1)}, bf16[2,40,5120]{2,1,0:T(8,128)(2,1)}, u32[]{:S(2)}) copy-start(bf16[2,40,5120]{2,1,0:T(8,128)(2,1)} %param.23) | copy-start | bytes 2457604
  0.0 8.9 %copy-start.6 = (bf16[2,40,1280]{2,1,0:T(8,128)(2,1)S(1)}, bf16[2,40,1280]{2,1,0:T(8,128)(2,1)}, u32[]{:S(2)}) copy-start(bf16[2,40,1280]{2,1,0:T(8,128)(2,1)} %param.20) | copy-start | bytes 614404
  0.0 8.1 %copy-start.5 = (bf16[2,40,1280]{2,1,0:T(8,128)(2,1)S(1)}, bf16[2,40,1280]{2,1,0:T(8,128)(2,1)}, u32[]{:S(2)}) copy-start(bf16[2,40,1280]{2,1,0:T(8,128)(2,1)} %param.19) | copy-start | bytes 614404
  0.9 8.6 %copy-start.7 = (bf16[2,40,1280]{2,1,0:T(8,128)(2,1)S(1)}, bf16[2,40,1280]{2,1,0:T(8,128)(2,1)}, u32[]{:S(2)}) copy-start(bf16[2,40,1280]{2,1,0:T(8,128)(2,1)} %param.21) | copy-start | bytes 614404
  0.9 9.4 %copy-start.8 = (bf16[2,40,1280]{2,1,0:T(8,128)(2,1)S(1)}, bf16[2,40,1280]{2,1,0:T(8,128)(2,1)}, u32[]{:S(2)}) copy-start(bf16[2,40,1280]{2,1,0:T(8,128)(2,1)} %param.22) | copy-start | bytes 614404
  3.5 9.4 %copy-start.4 = (bf16[2,40,5120]{2,1,0:T(8,128)(2,1)S(1)}, bf16[2,40,5120]{2,1,0:T(8,128)(2,1)}, u32[]{:S(2)}) copy-start(bf16[2,40,5120]{2,1,0:T(8,128)(2,1)} %param.25) | copy-start | bytes 2457604
  478.6 23.5 %copy-start.1 = (f32[32,1280]{1,0:T(8,128)S(1)}, f32[32,1280]{1,0:T(8,128)}, u32[]{:S(2)}) copy-start(f32[32,1280]{1,0:T(8,128)} %param.16) | copy-start | bytes 491524

commit v2 on v1

--- a/solution.py
+++ b/solution.py
@@ -89,9 +89,19 @@
     return plan
 
 
-def gather_kernel(lengths, layers, packed_ref, *refs):
-    full_refs = refs[:layers]
-    own_sem, send_sems, recv_sems = refs[layers:]
+def gather_kernel(lengths, layers, shard_count, *refs):
+    shard_refs, full_refs = refs[:shard_count], refs[shard_count : shard_count + layers]
+    packed_ref, pack_sem, own_sem, send_sems, recv_sems = refs[shard_count + layers :]
+    packing, column = [], 0
+    for index, shard_ref in enumerate(shard_refs):
+        size = shard_ref.shape[2]
+        packing.append(
+            pltpu.make_async_copy(
+                shard_ref, packed_ref.at[:, :, pl.ds(column, size)], pack_sem.at[index]
+            )
+        )
+        packing[-1].start()
+        column += size
     tp_count = lengths["z"]
     rep_here = lax.axis_index("rep")
     here = {
@@ -141,6 +151,8 @@
         count = count + (here[axis] < lengths[axis] - 1).astype(jnp.int32)
     pl.semaphore_wait(barrier, count)
 
+    for copy in packing:
+        copy.wait()
     my_rep, my_tp = device(here)
     own_copies = [
         pltpu.make_async_copy(
@@ -216,7 +228,7 @@
     for item in own:
         run(0, item)
     for layer in range(layers):
-        early = len(rest) // 2
+        early = len(rest) // 5
         for item in rest[:early]:
             run(layer, item)
         if layer + 1 < layers:
@@ -230,24 +242,28 @@
         copy.wait()
 
 
-def gather_weights(packed, rep_count, tp_count):
-    layers, rows, width = packed.shape
+def gather_weights(shards, rep_count, tp_count):
+    layers, rows, _ = shards[0].shape
+    width = sum(shard.shape[2] for shard in shards)
+    kind = shards[0].dtype
     devices = rep_count * tp_count
     lengths = {"x": 2, "y": rep_count // 4, "z": tp_count}
     slots = layers * sum(len(item[3]) + 1 for item in send_plan(lengths))
     full = pl.pallas_call(
-        functools.partial(gather_kernel, lengths, layers),
-        out_shape=[jax.ShapeDtypeStruct((devices, rows, width), packed.dtype)] * layers,
-        in_specs=[pl.BlockSpec(memory_space=pltpu.VMEM)],
+        functools.partial(gather_kernel, lengths, layers, len(shards)),
+        out_shape=[jax.ShapeDtypeStruct((devices, rows, width), kind)] * layers,
+        in_specs=[pl.BlockSpec(memory_space=pl.ANY)] * len(shards),
         out_specs=[pl.BlockSpec(memory_space=pl.ANY)] * layers,
         scratch_shapes=[
+            pltpu.VMEM((layers, rows, width), kind),
+            pltpu.SemaphoreType.DMA((len(shards),)),
             pltpu.SemaphoreType.DMA((layers,)),
             pltpu.SemaphoreType.DMA((slots,)),
             pltpu.SemaphoreType.DMA((layers * len(CLASSES), devices)),
         ],
         compiler_params=pltpu.CompilerParams(collective_id=0, has_side_effects=True),
         name="gather_weights",
-    )(packed)
+    )(*shards)
     return [one.reshape(devices * rows, width) for one in full]
 
 
@@ -282,6 +298,61 @@
     )
 
 
+def ffn_kernel(steps, stream_ref, gain_ref, gate_ref, up_ref, down_ref, out_ref, normed, total):
+    step = pl.program_id(0)
+
+    @pl.when(step == 0)
+    def _():
+        normed[...] = layer_norm(stream_ref[...], gain_ref[...])
+        total[...] = stream_ref[...]
+
+    gate_part = jnp.dot(normed[...], gate_ref[...], preferred_element_type=jnp.float32)
+    up_part = jnp.dot(normed[...], up_ref[...], preferred_element_type=jnp.float32)
+    gate_part = 0.5 * gate_part * (1.0 + lax.erf(gate_part * math.sqrt(0.5)))
+    hidden = (gate_part * up_part).astype(jnp.bfloat16)
+    total[...] += out_terms(hidden, down_ref[...])
+
+    @pl.when(step == steps - 1)
+    def _():
+        out_ref[...] = total[...].astype(out_ref.dtype)
+
+
+def feed_forward(stream, gain_vector, weights, first, inner, out_dtype):
+    rows, width = stream.shape
+    tile = 512 if inner % 512 == 0 and first % 512 == 0 else 128
+    steps = inner // tile
+    depth = weights.shape[0]
+
+    def columns(which):
+        base = (first + which * inner) // tile
+        return pl.BlockSpec((depth, tile), lambda step: (0, base + step))
+
+    return pl.pallas_call(
+        functools.partial(ffn_kernel, steps),
+        grid=(steps,),
+        out_shape=jax.ShapeDtypeStruct((rows, width), out_dtype),
+        in_specs=[
+            pl.BlockSpec((rows, width), lambda step: (0, 0)),
+            pl.BlockSpec((1, width), lambda step: (0, 0)),
+            columns(0),
+            columns(1),
+            columns(2),
+        ],
+        out_specs=pl.BlockSpec((rows, width), lambda step: (0, 0)),
+        scratch_shapes=[
+            pltpu.VMEM((rows, width), jnp.bfloat16),
+            pltpu.VMEM((rows, width), jnp.float32),
+        ],
+        compiler_params=pltpu.CompilerParams(dimension_semantics=("arbitrary",)),
+        cost_estimate=pl.CostEstimate(
+            flops=6 * rows * width * inner,
+            bytes_accessed=6 * depth * inner,
+            transcendentals=rows * inner,
+        ),
+        name="feed_forward",
+    )(stream, gain_vector[None], weights, weights, weights)
+
+
 def body(
     tokens,
     view_ids,
@@ -305,7 +376,7 @@
     shards = (w_query, w_key, w_value, w_out, w_gate, w_up, w_down)
     one_kernel = rep_count % 4 == 0 and rep_count * tp_count * LAYERS * len(CLASSES) <= 256
     if one_kernel:
-        weights = gather_weights(jnp.concatenate(shards, axis=2), rep_count, tp_count)
+        weights = gather_weights(shards, rep_count, tp_count)
     share_rows = tokens.shape[0]
     row_ids = lax.axis_index("tp") * share_rows + jnp.arange(share_rows, dtype=jnp.int32)
     stream = tokens.astype(jnp.float32) + conditioning(row_ids, view_ids, time_ids, camera_table)
@@ -325,6 +396,16 @@
         packed = jnp.dot(normed, qkv_w, preferred_element_type=jnp.float32).astype(jnp.bfloat16)
         mixed_rows = attend(packed, head_size)
         stream = stream + out_terms(mixed_rows, whole_weight(layer_index, 3, 1, mixed_rows))
+        if one_kernel:
+            stream = feed_forward(
+                stream,
+                norm_ffn[layer_index],
+                weights[layer_index],
+                4 * width,
+                inner,
+                jnp.bfloat16 if layer_index == LAYERS - 1 else jnp.float32,
+            )
+            continue
         normed = layer_norm(stream, norm_ffn[layer_index])
         gate_w = whole_weight(layer_index, 4, 1, normed)
         gate_part = jnp.dot(normed, gate_w, preferred_element_type=jnp.float32)

time: 512 us -> 470 us (0.918); the launches traced: 503 us -> 469 us
  matrix products: 99.7 us -> 31.7 us
  Pallas kernels: 386 us -> 427 us
  local copies, waits for them, and re-layouts: 11.6 us -> 4.93 us
    dot_general x4 -> x2, matrix products: 52.4 us -> 8.23 us  [out_terms(): lax.dot_general(mixed_rows, weight, (((1,), (1,)), ((), ())), preferred_e...]
    pallas_call x1 -> x3, Pallas kernels: 386 us -> 427 us  [the longest x1 384 us: gather_weights(): pl.pallas_call(functools.partial(gather_kernel, lengths, layers, len(shar...]
    dot_general x2 -> x0, matrix products: 21.7 us -> none  [body(): gate_part = jnp.dot(normed, gate_w, preferred_element_type=jnp.float32)]
where the time goes in v2:
time: 470 us; the launch traced here: 469 us
  Pallas kernels  427 us (91%)
  matrix products  31.7 us (7%)
  other arithmetic  5.37 us (1%)
  local copies, waits for them, and re-layouts  4.93 us (1%)
    pallas_call x1, Pallas kernels, gather_weights(): pl.pallas_call(functools.partial(gather_kernel, lengths, layers, len(shar...  384 us
    pallas_call x2, Pallas kernels, feed_forward(): pl.pallas_call(functools.partial(ffn_kernel, steps), grid=(steps,), out_s...  42.9 us
    dot_general x2, matrix products, body(): jnp.dot(normed, qkv_w, preferred_element_type=jnp.float32)  13.2 us

profile of v2, /device:TPU:0, one launch (start us, length us, event | category | flops | bytes accessed | tf_op | source)
XLA Modules:
  0.0 469.3 jit_solution(6148465108458620177)
XLA Ops:
  0.0 0.0 copy-start
  0.0 0.8 select_reduce_fusion.1
  0.8 2.3 multiply_cosine_fusion
  3.2 0.8 broadcast_in_dim.26
  3.9 0.1 select_reduce_fusion
  4.0 0.0 copy-done
  4.0 2.0 fusion.46
  6.0 0.0 copy-start.5
  6.1 384.2 %gather_weights.1 = (bf16[32,40,20480]{2,1,0:T(8,128)(2,1)}, bf16[32,40,20480]{2,1,0:T(8,128)(2,1)}) custom-call(bf16[2,40,1280]{2,1,0:T(8,128)(2,1)} %refs_0_.1, bf16[2,40,1280]{2,1,0:T(8,128)(2,1)} %refs_1_.1, bf16[2,40,1280]{2,1,0:T(8,128)(2,1)} %refs_2_.1, bf16[2,40,1280]{2,1,0:T(8,128)(2,1)} %refs_3_.1, bf16[2,40,5120]{2,1,0:T(8,128)(2,1)} %refs_4_.1, ...), custom_call_target="tpu_custom_call" | custom-call | tf_op jit(solution)/shard_map/gather_weights/pallas_call | solution.py:252
  390.3 0.0 copy-done.5
  390.4 0.3 multiply_reduce_fusion.3
  390.7 6.6 %fusion.6 = bf16[256,3840]{1,0:T(8,128)(2,1)S(1)} fusion(bf16[1280,20480]{1,0:T(8,128)(2,1)} %bitcast.32, f32[256,1280]{1,0:T(8,128)S(1)} %get-tuple-element.22, f32[1280]{0:T(1024)S(1)} %get-tuple-element.10, f32[256]{0:T(256)S(1)} %add_rsqrt_fusion.1, f32[256]{0:T(256)S(1)} %broadcast_multiply_fusion.1), kind=kOutput, calls=%fused_computation.6 | convolution fusion | flops 2518876160 | bytes 13114368 | tf_op jit(solution)/shard_map/dot_general | solution.py:396
  397.3 0.1 fusion.44
  397.4 1.1 copy.30
  398.5 0.2 copy.31
  398.7 0.2 copy.32
  399.0 0.0 copy-start.3
  399.0 2.2 fusion.47
  401.1 0.0 copy-done.3
  401.1 1.9 convolution_convert_fusion.1
  403.1 0.0 copy-start.6
  403.1 4.1 fusion.17.stream_ref
  407.2 0.0 copy-done.6
  407.2 0.6 fusion.45
  407.8 21.5 %feed_forward.2 = f32[256,1280]{1,0:T(8,128)} custom-call(f32[256,1280]{1,0:T(8,128)} %fusion.17.stream_ref, f32[1,1280]{1,0:T(1,128)} %get-tuple-element.18.gain_ref, bf16[1280,20480]{1,0:T(8,128)(2,1)} %bitcast.34, bf16[1280,20480]{1,0:T(8,128)(2,1)} %bitcast.35, bf16[1280,20480]{1,0:T(8,128)(2,1)} %bitcast.36), custom_call_target="tpu_custom_call" | custom-call | flops 10066329600 | bytes 39321600 | tf_op jit(solution)/shard_map/feed_forward/pallas_call | solution.py:330
  429.4 0.0 copy-start.2
  429.4 1.6 reduce_sum.77
  430.9 0.1 copy-done.2
  431.1 0.3 multiply_reduce_fusion.2
  431.4 6.6 %fusion.9 = bf16[256,3840]{1,0:T(8,128)(2,1)S(1)} fusion(bf16[1280,20480]{1,0:T(8,128)(2,1)} %bitcast.27, f32[256,1280]{1,0:T(8,128)S(1)} %copy-done.2, f32[1280]{0:T(1024)S(1)} %get-tuple-element.9, f32[256]{0:T(256)S(1)} %add_rsqrt_fusion, f32[256]{0:T(256)S(1)} %broadcast_multiply_fusion), kind=kOutput, calls=%fused_computation.7 | convolution fusion | flops 2518876160 | bytes 13114368 | tf_op jit(solution)/shard_map/dot_general | solution.py:396
  438.0 0.1 fusion.43
  438.1 1.1 copy.34
  439.2 0.2 copy.35
  439.4 0.2 copy.36
  439.7 0.0 copy-start.4
  439.7 2.2 fusion.48
  441.9 0.0 copy-done.4
  441.9 1.9 convolution_convert_fusion
  443.8 4.1 fusion.20.stream_ref
  448.0 0.0 copy-start.1
  448.0 21.3 %feed_forward.3 = bf16[256,1280]{1,0:T(8,128)(2,1)} custom-call(f32[256,1280]{1,0:T(8,128)} %fusion.20.stream_ref, f32[1,1280]{1,0:T(1,128)} %get-tuple-element.17.gain_ref, bf16[1280,20480]{1,0:T(8,128)(2,1)} %bitcast.29, bf16[1280,20480]{1,0:T(8,128)(2,1)} %bitcast.30, bf16[1280,20480]{1,0:T(8,128)(2,1)} %bitcast.31), custom_call_target="tpu_custom_call" | custom-call | flops 10066329600 | bytes 39321600 | tf_op jit(solution)/shard_map/feed_forward/pallas_call | solution.py:330
  469.3 0.0 copy-done.1
  (8 shorter events, 0.1 us)
Async XLA Ops:
  0.0 4.0 copy-start
  6.0 384.3 %copy-start.5 = (f32[2,1280]{1,0:T(2,128)S(1)}, f32[2,1280]{1,0:T(2,128)}, u32[]{:S(2)}) copy-start(f32[2,1280]{1,0:T(2,128)} %param.17) | copy-start | bytes 30724
  399.0 2.2 copy-start.3
  403.1 4.1 copy-start.6
  429.4 1.7 copy-start.2
  439.7 2.2 copy-start.4
  448.0 21.3 %copy-start.1 = (f32[32,1280]{1,0:T(8,128)S(1)}, f32[32,1280]{1,0:T(8,128)}, u32[]{:S(2)}) copy-start(f32[32,1280]{1,0:T(8,128)} %param.16) | copy-start | bytes 491524
